TPU v7x, 32 devices: a whole 2x2x4 slice. The times are simulated.
32 devices in a mesh: node: 8 (over y, x, core), grp: 4 (over z).
Axes of the slice: x: 2, y: 2, z: 4, core: 2. Of those that a mesh axis runs over, the one named last changes fastest.
Arguments:
- tokens: bfloat16 [12288, 1792], P(('node', 'grp')), may hold values from -6 to 6
- cotangent: bfloat16 [12288, 1792], P(('node', 'grp')), may hold values from -6 to 6
- gate_weight: bfloat16 [1792, 1024], P('node'), may hold values from -0.125 to 0.125
- up_weight: bfloat16 [1792, 1024], P('node'), may hold values from -0.125 to 0.125
- down_weight_t: bfloat16 [1792, 1024], P('node'), may hold values from -0.125 to 0.125
- error_memory: bfloat16 [4, 1792, 3072], P('grp', 'node'), may hold values from -4 to 4
- q_init: float32 [3, 1024, 32], replicated, may hold values from -6 to 6
Outputs:
- token_grad: bfloat16 [12288, 1792], P(('node', 'grp'))
- new_error: bfloat16 [4, 1792, 3072], P('grp', 'node')
- p_hat: float32 [3, 1792, 32], P(None, 'node')
- q_new: float32 [3, 1024, 32], replicated
All inputs are finite; a program needn't handle non-finite values.
Results may differ from a plain program's by a relative error of at most 0.012.
Values may be sent and summed in bfloat16 or wider, within the bound.
A program may use at most 192 MiB of HBM per device.

v0:
```python
import math
import jax
import jax.numpy as jnp
from jax import lax
from jax.sharding import PartitionSpec as P


def gelu_parts(value):
    coeff = math.sqrt(2.0 / math.pi)
    inner = coeff * (value + 0.044715 * value * value * value)
    tanh_value = jnp.tanh(inner)
    activation = 0.5 * value * (1.0 + tanh_value)
    slope = 0.5 * (1.0 + tanh_value) + 0.5 * value * (1.0 - tanh_value * tanh_value) * coeff * (
        1.0 + 3.0 * 0.044715 * value * value
    )
    return (activation, slope)


def contract_rows(left_side, right_side):
    return lax.dot_general(
        left_side, right_side, (((0,), (0,)), ((), ())), preferred_element_type=jnp.float32
    )


def on_device(tokens, cotangent, gate_weight, up_weight, down_weight_t, error_memory, q_init):
    node_count = lax.axis_size("node")
    group_count = lax.axis_size("grp")
    hidden_units = gate_weight.shape[1]
    highest = lax.Precision.HIGHEST
    full_gate, full_up, full_down = (
        lax.all_gather(gate_weight, "node", axis=0, tiled=True),
        lax.all_gather(up_weight, "node", axis=0, tiled=True),
        lax.all_gather(down_weight_t, "node", axis=0, tiled=True),
    )
    gate_pre = jnp.dot(tokens, full_gate, preferred_element_type=jnp.float32)
    up_pre = jnp.dot(tokens, full_up, preferred_element_type=jnp.float32)
    activation, slope = gelu_parts(gate_pre)
    hidden = (activation * up_pre).astype(jnp.bfloat16)
    back_hidden = jnp.dot(cotangent, full_down, preferred_element_type=jnp.float32)
    grad_up = (back_hidden * activation).astype(jnp.bfloat16)
    grad_gate = (back_hidden * up_pre * slope).astype(jnp.bfloat16)
    token_grad = (
        lax.dot_general(
            grad_gate, full_gate, (((1,), (1,)), ((), ())), preferred_element_type=jnp.float32
        )
        + lax.dot_general(
            grad_up, full_up, (((1,), (1,)), ((), ())), preferred_element_type=jnp.float32
        )
    ).astype(jnp.bfloat16)
    gate_up = jnp.concatenate([grad_gate, grad_up], axis=1)
    token_cols, cot_cols = (
        lax.all_to_all(tokens, "node", split_axis=1, concat_axis=0, tiled=True),
        lax.all_to_all(cotangent, "node", split_axis=1, concat_axis=0, tiled=True),
    )
    piece_gu = lax.all_gather(gate_up, "node", axis=0, tiled=True)
    piece_hidden = lax.all_gather(hidden, "node", axis=0, tiled=True)
    summed = jnp.concatenate(
        [contract_rows(token_cols, piece_gu), contract_rows(cot_cols, piece_hidden)], axis=1
    )
    grad_scale = 1.0 / math.sqrt(tokens.shape[0] * node_count)
    merged = summed * grad_scale + error_memory[0].astype(jnp.float32)
    blocks = [merged[:, m * hidden_units : (m + 1) * hidden_units] for m in range(3)]
    row_terms = jnp.stack([jnp.dot(blocks[m], q_init[m], precision=highest) for m in range(3)])
    power_rows = lax.psum(row_terms.astype(jnp.bfloat16), "grp").astype(jnp.float32) / group_count
    local_gram = jnp.einsum("mdr,mds->mrs", power_rows, power_rows, precision=highest)
    gram_matrix = lax.psum(local_gram, "node")
    hats = []
    for m in range(3):
        factor = jnp.linalg.cholesky(gram_matrix[m])
        hats.append(jax.scipy.linalg.solve_triangular(factor, power_rows[m].T, lower=True).T)
    col_terms = jnp.stack([jnp.dot(blocks[m].T, hats[m], precision=highest) for m in range(3)])
    q_new = lax.psum(col_terms, ("node", "grp")) / group_count
    errors = [blocks[m] - jnp.dot(hats[m], q_new[m].T, precision=highest) for m in range(3)]
    new_error = jnp.concatenate(errors, axis=1).astype(jnp.bfloat16)[None]
    return (token_grad, new_error, jnp.stack(hats), q_new)


def solution(mesh):
    return jax.shard_map(
        on_device,
        mesh=mesh,
        in_specs=(
            P(("node", "grp"), None),
            P(("node", "grp"), None),
            P("node", None),
            P("node", None),
            P("node", None),
            P("grp", "node", None),
            P(),
        ),
        out_specs=(P(("node", "grp"), None), P("grp", "node", None), P(None, "node", None), P()),
        check_vma=False,
    )
```

profile of v0, /device:TPU:0, one launch (start us, length us, event | category | flops | bytes accessed | tf_op | source)
XLA Modules:
  0.0 512.1 jit_solution(15546751805123783097)
XLA Ops:
  9.4 37.6 %all-gather.6.cloned.1.call-done = bf16[1792,1024]{1,0:T(8,128)(2,1)} async-done(((bf16[224,1024]{1,0:T(8,128)(2,1)}), bf16[1792,1024]{1,0:T(8,128)(2,1)}) %all-gather.6.cloned.1.call-update) | async-done | bytes 3670032 | tf_op jit(solution)/shard_map/all_gather | solution.py:33
  47.0 5.2 %fusion.44 = f32[384,1024]{1,0:T(8,128)} fusion(bf16[384,1792]{1,0:T(8,128)(2,1)} %param.11, bf16[1792,1024]{1,0:T(8,128)(2,1)} %all-gather.6.cloned.1.call-done), kind=kOutput, calls=%fused_computation.92 | convolution fusion | flops 1409286144 | bytes 6619136 | tf_op jit(solution)/shard_map/dot_general | solution.py:39
  52.2 31.1 %all-gather.10.cloned.1.call-done = bf16[1792,1024]{1,0:T(8,128)(2,1)} async-done(((bf16[224,1024]{1,0:T(8,128)(2,1)}), bf16[1792,1024]{1,0:T(8,128)(2,1)}) %all-gather.10.cloned.1.call-update) | async-done | bytes 3670032 | tf_op jit(solution)/shard_map/all_gather | solution.py:31
  83.3 4.8 fusion.45
  88.1 31.5 %all-gather.8.cloned.1.call-done = bf16[1792,1024]{1,0:T(8,128)(2,1)} async-done(((bf16[224,1024]{1,0:T(8,128)(2,1)}), bf16[1792,1024]{1,0:T(8,128)(2,1)}) %all-gather.8.cloned.1.call-update) | async-done | bytes 3670032 | tf_op jit(solution)/shard_map/all_gather | solution.py:32
  119.6 6.4 %multiply_convert_fusion = (bf16[384,1024]{1,0:T(8,128)(2,1)}, bf16[384,1024]{1,0:T(8,128)(2,1)S(1)}, bf16[384,1024]{1,0:T(8,128)(2,1)S(1)}) fusion(f32[384,1024]{1,0:T(8,128)} %fusion.45, f32[384,1024]{1,0:T(8,128)} %fusion.44, bf16[384,1792]{1,0:T(8,128)(2,1)S(1)} %copy-done.2, bf16[1792,1024]{1,0:T(8,128)(2,1)} %all-gather.8.cloned.1.call-done), kind=kOutput, calls=%fused_computation.15 | convolution fusion | flops 1419116544 | bytes 10551296 | tf_op jit(solution)/shard_map/dot_general | solution.py:36
  129.6 1.5 copy.17
  131.1 3.6 all-to-all-start.1
  134.7 1.5 copy.15
  136.3 24.3 %all-to-all-done.1 = bf16[384,8,224]{0,2,1:T(8,128)(2,1)S(1)} async-done(((bf16[384,8,224]{0,2,1:T(8,128)(2,1)}), bf16[384,8,224]{0,2,1:T(8,128)(2,1)S(1)}, u32[]{:S(2)}, u32[]{:S(2)}) %all-to-all-start.1) | async-done | bytes 1376288 | tf_op jit(solution)/shard_map/all_to_all | solution.py:53
  160.5 3.6 all-to-all-start
  165.7 31.9 %all-to-all-done = bf16[384,8,224]{0,2,1:T(8,128)(2,1)S(1)} async-done(((bf16[384,8,224]{0,2,1:T(8,128)(2,1)}), bf16[384,8,224]{0,2,1:T(8,128)(2,1)S(1)}, u32[]{:S(2)}, u32[]{:S(2)}) %all-to-all-start) | async-done | bytes 1376288 | tf_op jit(solution)/shard_map/all_to_all | solution.py:52
  198.9 5.4 %fusion.46 = f32[384,1792]{1,0:T(8,128)} fusion(bf16[384,1024]{1,0:T(8,128)(2,1)S(1)} %copy-done.8, bf16[1792,1024]{1,0:T(8,128)(2,1)} %all-gather.10.cloned.1.call-done), kind=kOutput, calls=%fused_computation.94 | convolution fusion | flops 1409286144 | bytes 7208960 | tf_op jit(solution)/shard_map/dot_general | solution.py:43
  204.3 5.4 %convolution_bitcast_fusion.1 = f32[224,1024]{1,0:T(8,128)} fusion(bf16[3072,224]{0,1:T(8,128)(2,1)S(1)} %bitcast.133, bf16[3072,1024]{1,0:T(8,128)(2,1)} %all-gather.14.cloned.1.call-done), kind=kOutput, calls=%fused_computation.19 | convolution fusion | flops 1409286144 | bytes 8585216 | tf_op jit(solution)/shard_map/dot_general | solution.py:20
  209.7 64.7 %all-gather.12.cloned.1.call-done = bf16[3072,2048]{1,0:T(8,128)(2,1)} async-done(((bf16[384,2048]{1,0:T(8,128)(2,1)}), bf16[3072,2048]{1,0:T(8,128)(2,1)}) %all-gather.12.cloned.1.call-update) | async-done | bytes 12582928 | tf_op jit(solution)/shard_map/all_gather | solution.py:55
  274.4 6.4 %convolution_bitcast_fusion = f32[224,2048]{1,0:T(8,128)S(1)} fusion(bf16[3072,224]{0,1:T(8,128)(2,1)S(1)} %bitcast.134, bf16[3072,2048]{1,0:T(8,128)(2,1)} %all-gather.12.cloned.1.call-done), kind=kOutput, calls=%fused_computation.4 | convolution fusion | flops 2818572288 | bytes 15794176 | tf_op jit(solution)/shard_map/dot_general | solution.py:20
  285.2 20.5 %psum.21 = bf16[3,224,32]{1,2,0:T(8,128)(2,1)} all-reduce(bf16[3,224,32]{1,2,0:T(8,128)(2,1)} %pad_maximum_fusion.4), channel_id=1, replica_groups=mesh['node'=8,'grp'=4] {'grp'}, use_global_device_ids=true, to_apply=%region_0.0 | all-reduce | flops 21504 | bytes 86016 | tf_op jit(solution)/shard_map/psum | solution.py:64
  305.6 1.7 fusion.33
  307.4 1.4 convert_multiply_fusion
  308.8 24.0 %psum.22 = f32[3,32,32]{1,2,0:T(8,128)} all-reduce(f32[3,32,32]{1,2,0:T(8,128)} %fusion.33), channel_id=1, replica_groups=mesh['node'=8,'grp'=4] {'node'}, use_global_device_ids=true, to_apply=%region_1.0 | all-reduce | flops 3072 | bytes 24576 | tf_op jit(solution)/shard_map/psum | solution.py:66
  339.2 3.6 cholesky.59
  344.8 3.8 custom-call.7
  348.5 3.6 cholesky.70
  354.1 3.2 custom-call.8
  357.3 1.6 fusion.32
  358.9 1.6 fusion.31
  360.5 3.6 cholesky.81
  366.0 3.2 custom-call.9
  370.9 1.4 convolution_bitcast_fusion.3
  373.8 5.7 %fusion = bf16[384,1792]{1,0:T(8,128)(2,1)} fusion(f32[384,1792]{1,0:T(8,128)} %fusion.46, bf16[384,1024]{1,0:T(8,128)(2,1)S(1)} %get-tuple-element.8, bf16[1792,1024]{1,0:T(8,128)(2,1)} %all-gather.8.cloned.1.call-done), kind=kOutput, calls=%fused_computation.1 | convolution fusion | flops 1410662400 | bytes 8585216 | tf_op jit(solution)/shard_map/dot_general | solution.py:46
  380.2 119.2 %all-reduce.2.cloned.1.call-done = f32[3,1024,32]{1,2,0:T(8,128)} async-done(((f32[3,1024,32]{1,2,0:T(8,128)}), f32[3,1024,32]{1,2,0:T(8,128)}) %all-reduce.2.cloned.1.call-update) | async-done | bytes 393232 | tf_op jit(solution)/shard_map/psum | solution.py:72
  500.4 1.8 fusion.12
  (78 shorter events, 33.0 us)
Async XLA Ops:
  7.2 39.8 %all-gather.6.cloned.1.call-start = ((), (), s32[]{:S(2)}) async-start(), calls=%async_computation.2 | async-start | bytes 4128768 | tf_op jit(solution)/shard_map/all_gather | solution.py:33
  7.9 75.4 %all-gather.10.cloned.1.call-start = ((), (), s32[]{:S(2)}) async-start(), calls=%async_computation.4 | async-start | bytes 4128768 | tf_op jit(solution)/shard_map/all_gather | solution.py:31
  8.6 111.0 %all-gather.8.cloned.1.call-start = ((), (), s32[]{:S(2)}) async-start(), calls=%async_computation.3 | async-start | bytes 4128768 | tf_op jit(solution)/shard_map/all_gather | solution.py:32
  9.4 73.9 %copy-start.2 = (bf16[384,1792]{1,0:T(8,128)(2,1)S(1)}, bf16[384,1792]{1,0:T(8,128)(2,1)}, u32[]{:S(2)}) copy-start(bf16[384,1792]{1,0:T(8,128)(2,1)} %param.10) | copy-start | bytes 4128772
  9.4 194.9 %all-gather.14.cloned.1.call-start = ((), (), s32[]{:S(2)}) async-start(), calls=%async_computation.6 | async-start | bytes 7077888 | tf_op jit(solution)/shard_map/all_gather | solution.py:56
  126.0 0.9 copy-start.7
  126.0 148.4 %all-gather.12.cloned.1.call-start = ((), (), s32[]{:S(2)}) async-start(), calls=%async_computation.5 | async-start | bytes 14155776 | tf_op jit(solution)/shard_map/all_gather | solution.py:55
  128.2 1.3 copy-start.1
  131.1 29.4 %all-to-all-start.1 = ((bf16[384,8,224]{0,2,1:T(8,128)(2,1)}), bf16[384,8,224]{0,2,1:T(8,128)(2,1)S(1)}, u32[]{:S(2)}, u32[]{:S(2)}) async-start(bf16[384,8,224]{0,2,1:T(8,128)(2,1)} %bitcast.3), calls=%async_computation.1 | async-start | bytes 2752512 | tf_op jit(solution)/shard_map/all_to_all | solution.py:53
  160.5 37.1 %all-to-all-start = ((bf16[384,8,224]{0,2,1:T(8,128)(2,1)}), bf16[384,8,224]{0,2,1:T(8,128)(2,1)S(1)}, u32[]{:S(2)}, u32[]{:S(2)}) async-start(bf16[384,8,224]{0,2,1:T(8,128)(2,1)} %bitcast), calls=%async_computation | async-start | bytes 2752512 | tf_op jit(solution)/shard_map/all_to_all | solution.py:52
  164.1 335.3 %all-reduce.2.cloned.1.call-start = ((), (), s32[]{:S(2)}) async-start(), calls=%async_computation.7 | async-start | bytes 786432 | tf_op jit(solution)/shard_map/psum | solution.py:72
  197.6 1.3 copy-start.8
  198.9 5.4 %copy-start.4 = (bf16[8,28,8,384]{3,2,0,1:T(8,128)(2,1)S(1)}, bf16[8,28,8,384]{3,2,0,1:T(8,128)(2,1)}, u32[]{:S(2)}) copy-start(bf16[8,28,8,384]{3,2,0,1:T(8,128)(2,1)} %copy.25) | copy-start | bytes 4128772
  204.3 70.1 %copy-start.5 = (bf16[8,28,8,384]{3,2,0,1:T(8,128)(2,1)S(1)}, bf16[8,28,8,384]{3,2,0,1:T(8,128)(2,1)}, u32[]{:S(2)}) copy-start(bf16[8,28,8,384]{3,2,0,1:T(8,128)(2,1)} %copy.24) | copy-start | bytes 4128772
  274.4 6.4 %copy-start.3 = (bf16[1,224,3072]{2,1,0:T(8,128)(2,1)S(1)}, bf16[1,224,3072]{2,1,0:T(8,128)(2,1)}, u32[]{:S(2)}) copy-start(bf16[1,224,3072]{2,1,0:T(8,128)(2,1)} %param.15) | copy-start | bytes 4128772
  274.4 6.4 %copy-start.6 = (f32[224,1024]{1,0:T(8,128)S(1)}, f32[224,1024]{1,0:T(8,128)}, u32[]{:S(2)}) copy-start(f32[224,1024]{1,0:T(8,128)} %convolution_bitcast_fusion.1) | copy-start | bytes 2752516
  280.8 1.0 copy-start.16
  369.2 3.1 copy-start.9
  370.2 2.8 copy-start.14
  373.8 5.7 %copy-start.10 = (f32[32,224]{1,0:T(8,128)S(1)}, f32[32,224]{1,0:T(8,128)}, u32[]{:S(2)}) copy-start(f32[32,224]{1,0:T(8,128)} %fusion.32) | copy-start | bytes 86020
  373.8 5.7 %copy-start.12 = (f32[32,224]{1,0:T(8,128)S(1)}, f32[32,224]{1,0:T(8,128)}, u32[]{:S(2)}) copy-start(f32[32,224]{1,0:T(8,128)} %fusion.31) | copy-start | bytes 86020
  373.8 5.7 %copy-start.15 = (f32[32,224]{1,0:T(8,128)S(1)}, f32[32,224]{1,0:T(8,128)}, u32[]{:S(2)}) copy-start(f32[32,224]{1,0:T(8,128)} %copy-done.14) | copy-start | bytes 86020
  379.5 122.7 %copy-start.13 = (f32[32,224]{1,0:T(8,128)S(1)}, f32[32,224]{1,0:T(8,128)}, u32[]{:S(2)}) copy-start(f32[32,224]{1,0:T(8,128)} %fusion.31) | copy-start | bytes 86020
  500.4 3.7 copy-start
  500.4 2.7 copy-start.11
Sparse Core Ops, SparseCore 0:
  9.9 37.0 all-gather.5
  48.9 34.3 all-gather.9
  85.2 34.3 all-gather.7
  126.1 74.4 all-gather.13
  202.4 71.9 all-gather.11
  373.9 125.4 all-reduce.1
where the time goes:
time: 514 us; the launch traced here: 512 us
  waiting for transfers between devices  342 us (67%)
  matrix products  54.2 us (11%)
  blocking collectives  44.5 us (9%)
  other arithmetic  35.7 us (7%)
  between operations  14.4 us (3%)
  local copies, waits for them, and re-layouts  13.4 us (3%)
  starting transfers between devices  7.6 us (1%)
    psum x1, waiting for transfers between devices, on_device(): q_new = lax.psum(col_terms, ('node', 'grp')) / group_count  119 us
    all_gather x1, waiting for transfers between devices, on_device(): piece_gu = lax.all_gather(gate_up, 'node', axis=0, tiled=True)  64.7 us
    all_gather x1, waiting for transfers between devices, on_device(): lax.all_gather(down_weight_t, 'node', axis=0, tiled=True)  37.6 us
    all_to_all x1, waiting for transfers between devices, on_device(): lax.all_to_all(tokens, 'node', split_axis=1, concat_axis=0, tiled=True)  31.9 us
    all_gather x1, waiting for transfers between devices, on_device(): lax.all_gather(up_weight, 'node', axis=0, tiled=True)  31.5 us
    all_gather x1, waiting for transfers between devices, on_device(): lax.all_gather(gate_weight, 'node', axis=0, tiled=True)  31.1 us
    all_to_all x1, waiting for transfers between devices, on_device(): lax.all_to_all(cotangent, 'node', split_axis=1, concat_axis=0, tiled=True)  24.3 us
    psum x1, blocking collectives, on_device(): gram_matrix = lax.psum(local_gram, 'node')  24 us
  transfers between devices with their start and end apart: 8, of which 7 were waited for; matrix products, arithmetic and copies ran while one was open for 7% of the time, Pallas kernels for 0%

commit v1 on v0

--- a/solution.py
+++ b/solution.py
@@ -69,7 +69,11 @@
         factor = jnp.linalg.cholesky(gram_matrix[m])
         hats.append(jax.scipy.linalg.solve_triangular(factor, power_rows[m].T, lower=True).T)
     col_terms = jnp.stack([jnp.dot(blocks[m].T, hats[m], precision=highest) for m in range(3)])
-    q_new = lax.psum(col_terms, ("node", "grp")) / group_count
+
+    def finish_tables_up(row_data, mesh_name):
+        return jnp.sum(lax.all_gather(row_data, mesh_name), 0)
+
+    q_new = finish_tables_up(col_terms, ("node", "grp")) / group_count
     errors = [blocks[m] - jnp.dot(hats[m], q_new[m].T, precision=highest) for m in range(3)]
     new_error = jnp.concatenate(errors, axis=1).astype(jnp.bfloat16)[None]
     return (token_grad, new_error, jnp.stack(hats), q_new)

time: 514 us -> 485 us (0.944)
  waiting for transfers between devices: 342 us -> 313 us
    psum x1 -> x0, waiting for transfers between devices: 119 us -> none  [on_device(): q_new = lax.psum(col_terms, ('node', 'grp')) / group_count]
    all_gather x0 -> x1, waiting for transfers between devices: none -> 84.6 us  [finish_tables_up(): return jnp.sum(lax.all_gather(row_data, mesh_name), 0)]
    reduce_sum x0 -> x1, other arithmetic: none -> 5.72 us  [finish_tables_up(): return jnp.sum(lax.all_gather(row_data, mesh_name), 0)]
  transfers between devices with their start and end apart: 8 -> 8, of which waited for: 7 -> 8; matrix products, arithmetic and copies ran while one was open for 7% -> 6% of each run, Pallas kernels for 0% -> 0%
where the time goes in v1:
time: 485 us; the launch traced here: 483 us
  waiting for transfers between devices  313 us (65%)
  matrix products  49.9 us (10%)
  blocking collectives  44.5 us (9%)
  other arithmetic  40.3 us (8%)
  between operations  14.4 us (3%)
  local copies, waits for them, and re-layouts  13.4 us (3%)
  starting transfers between devices  7.42 us (2%)
    all_gather x1, waiting for transfers between devices, finish_tables_up(): return jnp.sum(lax.all_gather(row_data, mesh_name), 0)  84.6 us
    all_gather x1, waiting for transfers between devices, on_device(): piece_gu = lax.all_gather(gate_up, 'node', axis=0, tiled=True)  68.4 us
    all_gather x1, waiting for transfers between devices, on_device(): lax.all_gather(down_weight_t, 'node', axis=0, tiled=True)  37.6 us
    all_to_all x1, waiting for transfers between devices, on_device(): lax.all_to_all(tokens, 'node', split_axis=1, concat_axis=0, tiled=True)  32.1 us
    all_gather x1, waiting for transfers between devices, on_device(): lax.all_gather(up_weight, 'node', axis=0, tiled=True)  31.5 us
    all_gather x1, waiting for transfers between devices, on_device(): lax.all_gather(gate_weight, 'node', axis=0, tiled=True)  31.1 us
    all_to_all x1, waiting for transfers between devices, on_device(): lax.all_to_all(cotangent, 'node', split_axis=1, concat_axis=0, tiled=True)  24.4 us
    psum x1, blocking collectives, on_device(): gram_matrix = lax.psum(local_gram, 'node')  24 us
  transfers between devices with their start and end apart: 8, of which 8 were waited for; matrix products, arithmetic and copies ran while one was open for 6% of the time, Pallas kernels for 0%

profile of v1, /device:TPU:0, one launch (start us, length us, event | category | flops | bytes accessed | tf_op | source)
XLA Modules:
  0.0 483.3 jit_solution(10899177169602629110)
XLA Ops:
  9.4 37.6 %all-gather.8.cloned.1.call-done = bf16[1792,1024]{1,0:T(8,128)(2,1)} async-done(((bf16[224,1024]{1,0:T(8,128)(2,1)}), bf16[1792,1024]{1,0:T(8,128)(2,1)}) %all-gather.8.cloned.1.call-update) | async-done | bytes 3670032 | tf_op jit(solution)/shard_map/all_gather | solution.py:33
  47.0 5.2 %fusion.44 = f32[384,1024]{1,0:T(8,128)} fusion(bf16[384,1792]{1,0:T(8,128)(2,1)} %param.11, bf16[1792,1024]{1,0:T(8,128)(2,1)} %all-gather.8.cloned.1.call-done), kind=kOutput, calls=%fused_computation.92 | convolution fusion | flops 1409286144 | bytes 6619136 | tf_op jit(solution)/shard_map/dot_general | solution.py:39
  52.2 31.1 %all-gather.12.cloned.1.call-done = bf16[1792,1024]{1,0:T(8,128)(2,1)} async-done(((bf16[224,1024]{1,0:T(8,128)(2,1)}), bf16[1792,1024]{1,0:T(8,128)(2,1)}) %all-gather.12.cloned.1.call-update) | async-done | bytes 3670032 | tf_op jit(solution)/shard_map/all_gather | solution.py:31
  83.3 4.8 fusion.45
  88.1 31.5 %all-gather.10.cloned.1.call-done = bf16[1792,1024]{1,0:T(8,128)(2,1)} async-done(((bf16[224,1024]{1,0:T(8,128)(2,1)}), bf16[1792,1024]{1,0:T(8,128)(2,1)}) %all-gather.10.cloned.1.call-update) | async-done | bytes 3670032 | tf_op jit(solution)/shard_map/all_gather | solution.py:32
  119.6 6.4 %multiply_convert_fusion = (bf16[384,1024]{1,0:T(8,128)(2,1)}, bf16[384,1024]{1,0:T(8,128)(2,1)S(1)}, bf16[384,1024]{1,0:T(8,128)(2,1)S(1)}) fusion(f32[384,1024]{1,0:T(8,128)} %fusion.45, f32[384,1024]{1,0:T(8,128)} %fusion.44, bf16[384,1792]{1,0:T(8,128)(2,1)S(1)} %copy-done.2, bf16[1792,1024]{1,0:T(8,128)(2,1)} %all-gather.10.cloned.1.call-done), kind=kOutput, calls=%fused_computation.15 | convolution fusion | flops 1419116544 | bytes 10551296 | tf_op jit(solution)/shard_map/dot_general | solution.py:36
  129.5 1.5 copy.25
  131.0 3.6 all-to-all-start.1
  134.6 1.5 copy.23
  136.1 24.4 %all-to-all-done.1 = bf16[384,8,224]{0,2,1:T(8,128)(2,1)S(1)} async-done(((bf16[384,8,224]{0,2,1:T(8,128)(2,1)}), bf16[384,8,224]{0,2,1:T(8,128)(2,1)S(1)}, u32[]{:S(2)}, u32[]{:S(2)}) %all-to-all-start.1) | async-done | bytes 1376288 | tf_op jit(solution)/shard_map/all_to_all | solution.py:53
  160.5 3.6 all-to-all-start
  165.5 32.1 %all-to-all-done = bf16[384,8,224]{0,2,1:T(8,128)(2,1)S(1)} async-done(((bf16[384,8,224]{0,2,1:T(8,128)(2,1)}), bf16[384,8,224]{0,2,1:T(8,128)(2,1)S(1)}, u32[]{:S(2)}, u32[]{:S(2)}) %all-to-all-start) | async-done | bytes 1376288 | tf_op jit(solution)/shard_map/all_to_all | solution.py:52
  198.9 1.8 all-gather.16.cloned.1.call-done
  200.7 5.4 %convolution_bitcast_fusion.1 = f32[224,1024]{1,0:T(8,128)} fusion(bf16[3072,224]{0,1:T(8,128)(2,1)S(1)} %bitcast.135, bf16[3072,1024]{1,0:T(8,128)(2,1)} %all-gather.16.cloned.1.call-done), kind=kOutput, calls=%fused_computation.19 | convolution fusion | flops 1409286144 | bytes 8585216 | tf_op jit(solution)/shard_map/dot_general | solution.py:20
  206.1 68.4 %all-gather.14.cloned.1.call-done = bf16[3072,2048]{1,0:T(8,128)(2,1)} async-done(((bf16[384,2048]{1,0:T(8,128)(2,1)}), bf16[3072,2048]{1,0:T(8,128)(2,1)}) %all-gather.14.cloned.1.call-update) | async-done | bytes 12582928 | tf_op jit(solution)/shard_map/all_gather | solution.py:55
  274.4 6.4 %convolution_bitcast_fusion = f32[224,2048]{1,0:T(8,128)S(1)} fusion(bf16[3072,224]{0,1:T(8,128)(2,1)S(1)} %bitcast.136, bf16[3072,2048]{1,0:T(8,128)(2,1)} %all-gather.14.cloned.1.call-done), kind=kOutput, calls=%fused_computation.4 | convolution fusion | flops 2818572288 | bytes 15794176 | tf_op jit(solution)/shard_map/dot_general | solution.py:20
  285.1 20.5 %psum.14 = bf16[3,224,32]{1,2,0:T(8,128)(2,1)} all-reduce(bf16[3,224,32]{1,2,0:T(8,128)(2,1)} %pad_maximum_fusion.4), channel_id=1, replica_groups=mesh['node'=8,'grp'=4] {'grp'}, use_global_device_ids=true, to_apply=%region_0.0 | all-reduce | flops 21504 | bytes 86016 | tf_op jit(solution)/shard_map/psum | solution.py:64
  305.6 1.7 fusion.33
  308.8 24.0 %psum.15 = f32[3,32,32]{1,2,0:T(8,128)} all-reduce(f32[3,32,32]{1,2,0:T(8,128)} %fusion.33), channel_id=1, replica_groups=mesh['node'=8,'grp'=4] {'node'}, use_global_device_ids=true, to_apply=%region_1.0 | all-reduce | flops 3072 | bytes 24576 | tf_op jit(solution)/shard_map/psum | solution.py:66
  339.1 3.6 cholesky.59
  344.7 3.8 custom-call.7
  348.5 3.6 cholesky.70
  354.1 3.2 custom-call.8
  357.2 1.6 fusion.32
  358.8 1.6 fusion.31
  360.4 3.6 cholesky.81
  366.0 3.2 custom-call.9
  373.8 4.0 fusion.46
  377.9 2.7 fusion
  381.2 84.6 %all-gather.18.cloned.1.call-done = f32[96,1024,32]{1,2,0:T(8,128)} async-done(((f32[3,1024,32]{1,2,0:T(8,128)}), f32[96,1024,32]{1,2,0:T(8,128)}) %all-gather.18.cloned.1.call-update) | async-done | bytes 12582928 | tf_op jit(solution)/shard_map/all_gather | solution.py:74
  465.9 5.7 %reduce_sum.9 = f32[3,1024,32]{1,2,0:T(8,128)S(1)} reduce(f32[32,3,1024,32]{2,3,1,0:T(8,128)} %bitcast.132, f32[]{:T(128)} %constant.49.clone.1), dimensions={0}, to_apply=%region_4.7 | reduce | flops 3047424 | bytes 12976132 | tf_op jit(solution)/shard_map/reduce_sum | solution.py:74
  471.7 1.8 fusion.12
  (79 shorter events, 34.5 us)
Async XLA Ops:
  7.2 39.8 %all-gather.8.cloned.1.call-start = ((), (), s32[]{:S(2)}) async-start(), calls=%async_computation.2 | async-start | bytes 4128768 | tf_op jit(solution)/shard_map/all_gather | solution.py:33
  7.9 75.4 %all-gather.12.cloned.1.call-start = ((), (), s32[]{:S(2)}) async-start(), calls=%async_computation.4 | async-start | bytes 4128768 | tf_op jit(solution)/shard_map/all_gather | solution.py:31
  8.6 111.0 %all-gather.10.cloned.1.call-start = ((), (), s32[]{:S(2)}) async-start(), calls=%async_computation.3 | async-start | bytes 4128768 | tf_op jit(solution)/shard_map/all_gather | solution.py:32
  9.4 73.9 %copy-start.2 = (bf16[384,1792]{1,0:T(8,128)(2,1)S(1)}, bf16[384,1792]{1,0:T(8,128)(2,1)}, u32[]{:S(2)}) copy-start(bf16[384,1792]{1,0:T(8,128)(2,1)} %param.10) | copy-start | bytes 4128772
  9.4 191.3 %all-gather.16.cloned.1.call-start = ((), (), s32[]{:S(2)}) async-start(), calls=%async_computation.6 | async-start | bytes 7077888 | tf_op jit(solution)/shard_map/all_gather | solution.py:56
  126.0 0.9 copy-start.7
  126.0 148.4 %all-gather.14.cloned.1.call-start = ((), (), s32[]{:S(2)}) async-start(), calls=%async_computation.5 | async-start | bytes 14155776 | tf_op jit(solution)/shard_map/all_gather | solution.py:55
  128.1 1.3 copy-start.1
  131.0 29.5 %all-to-all-start.1 = ((bf16[384,8,224]{0,2,1:T(8,128)(2,1)}), bf16[384,8,224]{0,2,1:T(8,128)(2,1)S(1)}, u32[]{:S(2)}, u32[]{:S(2)}) async-start(bf16[384,8,224]{0,2,1:T(8,128)(2,1)} %bitcast.3), calls=%async_computation.1 | async-start | bytes 2752512 | tf_op jit(solution)/shard_map/all_to_all | solution.py:53
  160.5 37.1 %all-to-all-start = ((bf16[384,8,224]{0,2,1:T(8,128)(2,1)}), bf16[384,8,224]{0,2,1:T(8,128)(2,1)S(1)}, u32[]{:S(2)}, u32[]{:S(2)}) async-start(bf16[384,8,224]{0,2,1:T(8,128)(2,1)} %bitcast), calls=%async_computation | async-start | bytes 2752512 | tf_op jit(solution)/shard_map/all_to_all | solution.py:52
  164.1 301.8 %all-gather.18.cloned.1.call-start = ((), (), s32[]{:S(2)}) async-start(), calls=%async_computation.7 | async-start | bytes 12976128 | tf_op jit(solution)/shard_map/all_gather | solution.py:74
  165.5 35.2 %copy-start.4 = (bf16[8,28,8,384]{3,2,0,1:T(8,128)(2,1)S(1)}, bf16[8,28,8,384]{3,2,0,1:T(8,128)(2,1)}, u32[]{:S(2)}) copy-start(bf16[8,28,8,384]{3,2,0,1:T(8,128)(2,1)} %copy.33) | copy-start | bytes 4128772
  200.6 73.8 %copy-start.5 = (bf16[8,28,8,384]{3,2,0,1:T(8,128)(2,1)S(1)}, bf16[8,28,8,384]{3,2,0,1:T(8,128)(2,1)}, u32[]{:S(2)}) copy-start(bf16[8,28,8,384]{3,2,0,1:T(8,128)(2,1)} %copy.32) | copy-start | bytes 4128772
  274.4 6.4 %copy-start.3 = (bf16[1,224,3072]{2,1,0:T(8,128)(2,1)S(1)}, bf16[1,224,3072]{2,1,0:T(8,128)(2,1)}, u32[]{:S(2)}) copy-start(bf16[1,224,3072]{2,1,0:T(8,128)(2,1)} %param.15) | copy-start | bytes 4128772
  274.4 6.4 %copy-start.6 = (f32[224,1024]{1,0:T(8,128)S(1)}, f32[224,1024]{1,0:T(8,128)}, u32[]{:S(2)}) copy-start(f32[224,1024]{1,0:T(8,128)} %convolution_bitcast_fusion.1) | copy-start | bytes 2752516
  280.8 1.0 copy-start.15
  369.1 3.1 copy-start.8
  370.2 2.8 copy-start.13
  373.8 4.1 copy-start.16
  377.8 2.7 copy-start.9
  377.9 2.7 copy-start.11
  377.9 2.7 copy-start.14
  471.6 1.8 copy-start.12
  471.6 3.7 copy-start
  471.6 2.7 copy-start.10
Sparse Core Ops, SparseCore 0:
  9.9 37.0 all-gather.7
  48.9 34.3 all-gather.11
  85.2 34.3 all-gather.9
  126.1 74.4 all-gather.15
  202.4 71.9 all-gather.13
  373.9 91.9 all-gather.17
